TPU v7x, 32 devices: a whole 2x2x4 slice. The times are simulated.
32 devices in a mesh: gx: 8 (over y, x, core), gy: 4 (over z).
Axes of the slice: x: 2, y: 2, z: 4, core: 2. Of those that a mesh axis runs over, the one named last changes fastest.
Arguments:
- layer_early: bfloat16 [1024, 8192], P(None, ('gx', 'gy')), may hold values from -48 to 48
- layer_late: bfloat16 [1024, 8192], P(('gx', 'gy')), may hold values from -48 to 48
Outputs:
- similarity: float32 [], replicated
- token_share: float32 [1024], P(('gx', 'gy'))
- early_rows: bfloat16 [1024, 8192], P(('gx', 'gy'))
- late_rows: bfloat16 [1024, 8192], P(('gx', 'gy'))
All inputs are finite; a program needn't handle non-finite values.
Results may differ from a plain program's by a relative error of at most 0.0015.
Values may be sent and summed in bfloat16 or wider, within the bound.
A program may use at most 128 MiB of HBM per device.

v0:
```python
import jax
import jax.numpy as jnp
from jax import lax
from jax.sharding import PartitionSpec as P


def pair_terms(left_early, left_late, right_early, right_late):
    dims = (((1,), (1,)), ((), ()))
    block_early = lax.dot_general(left_early, right_early, dims, preferred_element_type=jnp.float32)
    block_late = lax.dot_general(left_late, right_late, dims, preferred_element_type=jnp.float32)
    return (
        jnp.sum(block_early * block_late, axis=1),
        jnp.sum(block_early * block_early),
        jnp.sum(block_late * block_late),
    )


def body(layer_early, layer_late):
    total_rows = layer_early.shape[0]
    early_values = layer_early.astype(jnp.float32)
    early_cols = (early_values - jnp.mean(early_values, axis=0)).astype(jnp.bfloat16)
    late_values = layer_late.astype(jnp.float32)
    column_sums = lax.psum(jnp.sum(late_values, axis=0), ("gx", "gy"))
    late_rows = (late_values - column_sums / total_rows).astype(jnp.bfloat16)
    early_rows = lax.all_to_all(early_cols, ("gx", "gy"), split_axis=0, concat_axis=1, tiled=True)
    block_early, block_late = (
        lax.all_gather(early_rows, "gy", axis=0, tiled=True),
        lax.all_gather(late_rows, "gy", axis=0, tiled=True),
    )
    row_part, early_part, late_part = pair_terms(
        block_early,
        block_late,
        lax.all_gather(early_rows, "gx", axis=0, tiled=True),
        lax.all_gather(late_rows, "gx", axis=0, tiled=True),
    )
    own_align = lax.psum_scatter(row_part, "gy", scatter_dimension=0, tiled=True)
    total_kl, total_kk, total_ll = lax.psum(
        (jnp.sum(row_part), early_part, late_part), ("gx", "gy")
    )
    scale_norm = jnp.sqrt(total_kk * total_ll)
    similarity = total_kl / scale_norm
    token_share = total_rows * own_align / scale_norm
    return (similarity, token_share, early_rows, late_rows)


def solution(mesh):
    in_specs = (P(None, ("gx", "gy")), P(("gx", "gy"), None))
    out_specs = (P(), P(("gx", "gy")), P(("gx", "gy"), None), P(("gx", "gy"), None))
    return jax.shard_map(body, mesh=mesh, in_specs=in_specs, out_specs=out_specs, check_vma=False)
```

profile of v0, /device:TPU:0, one launch (start us, length us, event | category | flops | bytes accessed | tf_op | source)
XLA Modules:
  0.0 298.2 jit_solution(8457581897998979989)
XLA Ops:
  7.2 0.0 copy-start
  7.2 0.0 all-gather.9.cloned.1.call-start
  7.2 1.2 convert_reduce_fusion
  8.4 42.1 %psum.28 = f32[8192]{0:T(1024)S(1)} all-reduce(f32[8192]{0:T(1024)S(1)} %convert_reduce_fusion), channel_id=1, replica_groups=mesh['gx'=8,'gy'=4] {'gx','gy'}, use_global_device_ids=true, to_apply=%region_2.0 | all-reduce | flops 8192 | bytes 65536 | tf_op jit(solution)/shard_map/psum | solution.py:23
  50.6 1.9 fusion.1
  52.5 0.0 all-gather.9.cloned.1.call-update
  52.5 0.0 all-gather.11.cloned.1.call-start
  52.5 0.7 all-gather.11.cloned.1.call-update
  53.3 0.0 all-gather.5.cloned.1.call-start
  53.3 1.2 convert_reduce_fusion.1
  54.5 1.1 fusion
  55.6 28.2 %all_to_all.19 = bf16[32,32,256]{2,1,0:T(8,128)(2,1)S(1)} all-to-all(bf16[32,32,256]{2,1,0:T(8,128)(2,1)S(1)} %bitcast.12), channel_id=1, replica_groups=mesh['gx'=8,'gy'=4] {'gx','gy'}, dimensions={0} | all-to-all | bytes 1048576 | tf_op jit(solution)/shard_map/all_to_all | solution.py:25
  83.9 0.8 copy.8
  84.7 0.0 all-gather.5.cloned.1.call-update
  84.7 0.0 all-gather.7.cloned.1.call-start
  84.8 0.5 all-gather.7.cloned.1.call-update
  85.3 0.0 copy-done
  85.3 0.6 dynamic-slice
  86.6 22.4 %all-gather.9.cloned.1.call-done = bf16[128,8192]{1,0:T(8,128)(2,1)} async-done(((bf16[32,8192]{1,0:T(8,128)(2,1)}), bf16[128,8192]{1,0:T(8,128)(2,1)}) %all-gather.9.cloned.1.call-update) | async-done | bytes 2097168 | tf_op jit(solution)/shard_map/all_gather | solution.py:28
  109.0 38.1 %all-gather.11.cloned.1.call-done = bf16[256,8192]{1,0:T(8,128)(2,1)} async-done(((bf16[32,8192]{1,0:T(8,128)(2,1)}), bf16[256,8192]{1,0:T(8,128)(2,1)}) %all-gather.11.cloned.1.call-update) | async-done | bytes 4194320 | tf_op jit(solution)/shard_map/all_gather | solution.py:34
  147.1 4.4 %fusion.3 = f32[128,256]{1,0:T(8,128)S(1)} fusion(bf16[128,8192]{1,0:T(8,128)(2,1)} %all-gather.9.cloned.1.call-done, bf16[256,8192]{1,0:T(8,128)(2,1)} %all-gather.11.cloned.1.call-done), kind=kOutput, calls=%fused_computation.14 | convolution fusion | flops 536870912 | bytes 6422528 | tf_op jit(solution)/shard_map/dot_general | solution.py:10
  151.5 43.5 %all-gather.5.cloned.1.call-done = bf16[128,8192]{1,0:T(8,128)(2,1)} async-done(((bf16[32,8192]{1,0:T(8,128)(2,1)}), bf16[128,8192]{1,0:T(8,128)(2,1)}) %all-gather.5.cloned.1.call-update) | async-done | bytes 2097168 | tf_op jit(solution)/shard_map/all_gather | solution.py:27
  195.0 37.7 %all-gather.7.cloned.1.call-done = bf16[256,8192]{1,0:T(8,128)(2,1)} async-done(((bf16[32,8192]{1,0:T(8,128)(2,1)}), bf16[256,8192]{1,0:T(8,128)(2,1)}) %all-gather.7.cloned.1.call-update) | async-done | bytes 4194320 | tf_op jit(solution)/shard_map/all_gather | solution.py:33
  232.7 5.0 %multiply_reduce_fusion.2 = (f32[128]{0:T(128)S(1)}, f32[]{:T(128)}, f32[]{:T(128)}, f32[]{:T(128)}) fusion(f32[128,256]{1,0:T(8,128)S(1)} %fusion.3, bf16[128,8192]{1,0:T(8,128)(2,1)} %all-gather.5.cloned.1.call-done, bf16[256,8192]{1,0:T(8,128)(2,1)} %all-gather.7.cloned.1.call-done), kind=kOutput, calls=%fused_computation.8 | convolution fusion | flops 537100160 | bytes 6423052 | tf_op jit(solution)/shard_map/dot_general | solution.py:9
  237.7 39.6 %all-reduce.1 = (f32[]{:T(128)}, f32[]{:T(128)}, f32[]{:T(128)}) all-reduce(f32[]{:T(128)} %get-tuple-element.5, f32[]{:T(128)} %get-tuple-element.7, f32[]{:T(128)} %get-tuple-element.6), channel_id=1, replica_groups=mesh['gx'=8,'gy'=4] {'gx','gy'}, use_global_device_ids=true, to_apply=%region_4.0 | all-reduce | flops 3 | bytes 24 | tf_op jit(solution)/shard_map/psum | solution.py:37
  278.7 10.6 %all-reduce = f32[128]{0:T(128)S(1)} all-reduce(f32[128]{0:T(128)S(1)} %get-tuple-element.4), channel_id=2, replica_groups=mesh['gx'=8,'gy'=4] {'gy'}, use_global_device_ids=true, to_apply=%region_10.0.clone | all-reduce | flops 128 | bytes 1024
  290.0 0.6 fusion.2
  (2 shorter events, 0.0 us)
Async XLA Ops:
  7.2 78.2 %copy-start = (u32[32]{0:T(128)S(1)}, u32[32]{0:T(128)}, u32[]{:S(2)}) copy-start(u32[32]{0:T(128)} %constant.11) | copy-start | bytes 388
  7.2 101.8 %all-gather.9.cloned.1.call-start = ((), (), s32[]{:S(2)}) async-start(), calls=%async_computation.3 | async-start | bytes 2621440 | tf_op jit(solution)/shard_map/all_gather | solution.py:28
  52.5 94.6 %all-gather.11.cloned.1.call-start = ((), (), s32[]{:S(2)}) async-start(), calls=%async_computation.4 | async-start | bytes 4718592 | tf_op jit(solution)/shard_map/all_gather | solution.py:34
  53.3 141.7 %all-gather.5.cloned.1.call-start = ((), (), s32[]{:S(2)}) async-start(), calls=%async_computation.1 | async-start | bytes 2621440 | tf_op jit(solution)/shard_map/all_gather | solution.py:27
  84.7 147.9 %all-gather.7.cloned.1.call-start = ((), (), s32[]{:S(2)}) async-start(), calls=%async_computation.2 | async-start | bytes 4718592 | tf_op jit(solution)/shard_map/all_gather | solution.py:33
Sparse Core Ops, SparseCore 0:
  52.6 56.3 all-gather.8
  111.5 35.5 all-gather.10
  149.3 45.6 all-gather.4
  197.3 35.3 all-gather.6
where the time goes:
time: 299 us; the launch traced here: 298 us
  waiting for transfers between devices  143 us (48%)
  blocking collectives  121 us (40%)
  between operations  17.6 us (6%)
  matrix products  9.4 us (3%)
  other arithmetic  6.03 us (2%)
    all_gather x1, waiting for transfers between devices, body(): lax.all_gather(early_rows, 'gy', axis=0, tiled=True)  43.5 us
    psum x1, blocking collectives, body(): column_sums = lax.psum(jnp.sum(late_values, axis=0), ('gx', 'gy'))  42.1 us
    psum x1, blocking collectives, body(): lax.psum((jnp.sum(row_part), early_part, late_part), ('gx', 'gy'))  39.6 us
    all_gather x1, waiting for transfers between devices, body(): lax.all_gather(late_rows, 'gx', axis=0, tiled=True)  38.1 us
    all_gather x1, waiting for transfers between devices, body(): lax.all_gather(early_rows, 'gx', axis=0, tiled=True)  37.7 us
    all_to_all x1, blocking collectives, body(): lax.all_to_all(early_cols, ('gx', 'gy'), split_axis=0, concat_axis=1, til...  28.2 us
    all_gather x1, waiting for transfers between devices, body(): lax.all_gather(late_rows, 'gy', axis=0, tiled=True)  22.4 us
    unnamed x1, blocking collectives  10.6 us
  transfers between devices with their start and end apart: 4, of which 4 were waited for; matrix products, arithmetic and copies ran while one was open for 3% of the time, Pallas kernels for 0%

commit v1 on v0

--- a/solution.py
+++ b/solution.py
@@ -22,7 +22,9 @@
     late_values = layer_late.astype(jnp.float32)
     column_sums = lax.psum(jnp.sum(late_values, axis=0), ("gx", "gy"))
     late_rows = (late_values - column_sums / total_rows).astype(jnp.bfloat16)
-    early_rows = lax.all_to_all(early_cols, ("gx", "gy"), split_axis=0, concat_axis=1, tiled=True)
+    shards = jnp.split(early_cols, lax.axis_size(("gx", "gy")), axis=0)
+    incoming = lax.all_to_all(jnp.stack(shards), ("gx", "gy"), 0, 0)
+    early_rows = jnp.concatenate(incoming, axis=1)
     block_early, block_late = (
         lax.all_gather(early_rows, "gy", axis=0, tiled=True),
         lax.all_gather(late_rows, "gy", axis=0, tiled=True),

time: 299 us -> 299 us (level)
  waiting for transfers between devices: 143 us -> 140 us
where the time goes in v1:
time: 299 us; the launch traced here: 298 us
  waiting for transfers between devices  140 us (47%)
  blocking collectives  123 us (41%)
  between operations  17.9 us (6%)
  matrix products  9.4 us (3%)
  other arithmetic  6.03 us (2%)
    all_gather x1, waiting for transfers between devices, body(): lax.all_gather(early_rows, 'gy', axis=0, tiled=True)  43.5 us
    psum x1, blocking collectives, body(): column_sums = lax.psum(jnp.sum(late_values, axis=0), ('gx', 'gy'))  42.1 us
    psum x1, blocking collectives, body(): lax.psum((jnp.sum(row_part), early_part, late_part), ('gx', 'gy'))  39.6 us
    all_gather x1, waiting for transfers between devices, body(): lax.all_gather(late_rows, 'gx', axis=0, tiled=True)  37.8 us
    all_gather x1, waiting for transfers between devices, body(): lax.all_gather(early_rows, 'gx', axis=0, tiled=True)  37.7 us
    all_to_all x1, blocking collectives, body(): incoming = lax.all_to_all(jnp.stack(shards), ('gx', 'gy'), 0, 0)  30.6 us
    all_gather x1, waiting for transfers between devices, body(): lax.all_gather(late_rows, 'gy', axis=0, tiled=True)  20.1 us
    unnamed x1, blocking collectives  10.6 us
  transfers between devices with their start and end apart: 4, of which 4 were waited for; matrix products, arithmetic and copies ran while one was open for 3% of the time, Pallas kernels for 0%

profile of v1, /device:TPU:0, one launch (start us, length us, event | category | flops | bytes accessed | tf_op | source)
XLA Modules:
  0.0 298.3 jit_solution(7248487822186111369)
XLA Ops:
  7.2 0.0 copy-start
  7.2 0.0 all-gather.9.cloned.1.call-start
  7.2 1.2 convert_reduce_fusion
  8.4 42.1 %psum.28 = f32[8192]{0:T(1024)S(1)} all-reduce(f32[8192]{0:T(1024)S(1)} %convert_reduce_fusion), channel_id=1, replica_groups=mesh['gx'=8,'gy'=4] {'gx','gy'}, use_global_device_ids=true, to_apply=%region_2.0 | all-reduce | flops 8192 | bytes 65536 | tf_op jit(solution)/shard_map/psum | solution.py:23
  50.6 1.9 fusion.1
  52.5 0.0 all-gather.9.cloned.1.call-update
  52.5 0.0 all-gather.11.cloned.1.call-start
  52.5 0.7 all-gather.11.cloned.1.call-update
  53.3 0.0 all-gather.5.cloned.1.call-start
  53.3 1.2 convert_reduce_fusion.1
  54.5 1.1 fusion
  56.0 30.6 %all_to_all.5 = bf16[32,32,256]{2,1,0:T(8,128)(2,1)S(1)} all-to-all(bf16[32,32,256]{2,1,0:T(8,128)(2,1)S(1)} %constant_dynamic-update-slice_fusion), channel_id=1, replica_groups=mesh['gx'=8,'gy'=4] {'gx','gy'}, dimensions={0} | all-to-all | bytes 1048576 | tf_op jit(solution)/shard_map/all_to_all | solution.py:26
  86.6 0.8 copy.8
  87.4 0.0 all-gather.5.cloned.1.call-update
  87.4 0.0 all-gather.7.cloned.1.call-start
  87.5 0.5 all-gather.7.cloned.1.call-update
  88.0 0.0 copy-done
  88.0 0.6 dynamic-slice
  89.3 20.1 %all-gather.9.cloned.1.call-done = bf16[128,8192]{1,0:T(8,128)(2,1)} async-done(((bf16[32,8192]{1,0:T(8,128)(2,1)}), bf16[128,8192]{1,0:T(8,128)(2,1)}) %all-gather.9.cloned.1.call-update) | async-done | bytes 2097168 | tf_op jit(solution)/shard_map/all_gather | solution.py:30
  109.4 37.8 %all-gather.11.cloned.1.call-done = bf16[256,8192]{1,0:T(8,128)(2,1)} async-done(((bf16[32,8192]{1,0:T(8,128)(2,1)}), bf16[256,8192]{1,0:T(8,128)(2,1)}) %all-gather.11.cloned.1.call-update) | async-done | bytes 4194320 | tf_op jit(solution)/shard_map/all_gather | solution.py:36
  147.2 4.4 %fusion.3 = f32[128,256]{1,0:T(8,128)S(1)} fusion(bf16[128,8192]{1,0:T(8,128)(2,1)} %all-gather.9.cloned.1.call-done, bf16[256,8192]{1,0:T(8,128)(2,1)} %all-gather.11.cloned.1.call-done), kind=kOutput, calls=%fused_computation.78 | convolution fusion | flops 536870912 | bytes 6422528 | tf_op jit(solution)/shard_map/dot_general | solution.py:10
  151.6 43.5 %all-gather.5.cloned.1.call-done = bf16[128,8192]{1,0:T(8,128)(2,1)} async-done(((bf16[32,8192]{1,0:T(8,128)(2,1)}), bf16[128,8192]{1,0:T(8,128)(2,1)}) %all-gather.5.cloned.1.call-update) | async-done | bytes 2097168 | tf_op jit(solution)/shard_map/all_gather | solution.py:29
  195.1 37.7 %all-gather.7.cloned.1.call-done = bf16[256,8192]{1,0:T(8,128)(2,1)} async-done(((bf16[32,8192]{1,0:T(8,128)(2,1)}), bf16[256,8192]{1,0:T(8,128)(2,1)}) %all-gather.7.cloned.1.call-update) | async-done | bytes 4194320 | tf_op jit(solution)/shard_map/all_gather | solution.py:35
  232.8 5.0 %multiply_reduce_fusion.2 = (f32[128]{0:T(128)S(1)}, f32[]{:T(128)}, f32[]{:T(128)}, f32[]{:T(128)}) fusion(f32[128,256]{1,0:T(8,128)S(1)} %fusion.3, bf16[128,8192]{1,0:T(8,128)(2,1)} %all-gather.5.cloned.1.call-done, bf16[256,8192]{1,0:T(8,128)(2,1)} %all-gather.7.cloned.1.call-done), kind=kOutput, calls=%fused_computation.40 | convolution fusion | flops 537100160 | bytes 6423052 | tf_op jit(solution)/shard_map/dot_general | solution.py:9
  237.8 39.6 %all-reduce.1 = (f32[]{:T(128)}, f32[]{:T(128)}, f32[]{:T(128)}) all-reduce(f32[]{:T(128)} %get-tuple-element.5, f32[]{:T(128)} %get-tuple-element.7, f32[]{:T(128)} %get-tuple-element.6), channel_id=1, replica_groups=mesh['gx'=8,'gy'=4] {'gx','gy'}, use_global_device_ids=true, to_apply=%region_4.0 | all-reduce | flops 3 | bytes 24 | tf_op jit(solution)/shard_map/psum | solution.py:39
  278.8 10.6 %all-reduce = f32[128]{0:T(128)S(1)} all-reduce(f32[128]{0:T(128)S(1)} %get-tuple-element.4), channel_id=2, replica_groups=mesh['gx'=8,'gy'=4] {'gy'}, use_global_device_ids=true, to_apply=%region_10.0.clone | all-reduce | flops 128 | bytes 1024
  290.1 0.6 fusion.2
  (34 shorter events, 0.1 us)
Async XLA Ops:
  7.2 80.9 %copy-start = (u32[32]{0:T(128)S(1)}, u32[32]{0:T(128)}, u32[]{:S(2)}) copy-start(u32[32]{0:T(128)} %constant.11) | copy-start | bytes 388
  7.2 102.2 %all-gather.9.cloned.1.call-start = ((), (), s32[]{:S(2)}) async-start(), calls=%async_computation.3 | async-start | bytes 2621440 | tf_op jit(solution)/shard_map/all_gather | solution.py:30
  52.5 94.7 %all-gather.11.cloned.1.call-start = ((), (), s32[]{:S(2)}) async-start(), calls=%async_computation.4 | async-start | bytes 4718592 | tf_op jit(solution)/shard_map/all_gather | solution.py:36
  53.3 141.8 %all-gather.5.cloned.1.call-start = ((), (), s32[]{:S(2)}) async-start(), calls=%async_computation.1 | async-start | bytes 2621440 | tf_op jit(solution)/shard_map/all_gather | solution.py:29
  87.4 145.4 %all-gather.7.cloned.1.call-start = ((), (), s32[]{:S(2)}) async-start(), calls=%async_computation.2 | async-start | bytes 4718592 | tf_op jit(solution)/shard_map/all_gather | solution.py:35
Sparse Core Ops, SparseCore 0:
  52.6 56.7 all-gather.8
  111.8 35.3 all-gather.10
  149.4 45.6 all-gather.4
  197.4 35.3 all-gather.6
